TPU v7x, 256 devices: a whole 4x4x8 slice. The times are simulated.
256 devices in a mesh: dp: 64 (over y_hi, z, x), mp: 4 (over y_lo, core).
Axes of the slice: x: 4, y: 4 (y_hi: 2, y_lo: 2; y = y_hi * 2 + y_lo), z: 8, core: 2. Of those that a mesh axis runs over, the one named last changes fastest.
Arguments:
- observations: bfloat16 [212992, 2048], P('dp', 'mp'), may hold values from -140 to 140
- layer_weights: bfloat16 [2, 2048, 2048], P(None, 'dp', 'mp'), may hold values from -0.1875 to 0.1875
- head_weights: bfloat16 [2048, 18], P('mp'), may hold values from -0.1875 to 0.1875
- rewards: float32 [3328, 64], P('dp'), may hold values from -6 to 6
- actions: int32 [3328, 64], P('dp'), may hold values from 0 to 17
- done_flags: int32 [3328, 64], P('dp'), may hold values 0 or 1
- behaviour: float32 [3328, 64], P('dp'), may hold values from 0.05 to 1
Outputs:
- targets: float32 [3328, 64], P('dp')
All inputs are finite; a program needn't handle non-finite values. No bound on the sum of `done_flags` on one device may be relied on, other than what follows from the above.
Results may differ from a plain program's by a relative error of at most 0.0056.
Values may be sent and summed in bfloat16 or wider, within the bound.
A program may use at most 128 MiB of HBM per device.

v0:
```python
import jax
import jax.numpy as jnp
from jax import lax
from jax.sharding import Mesh
from jax.sharding import PartitionSpec as P

DP = ("dp_0", "dp_1", "dp_2")


def laid_out(tiles, dim):
    tiles = jnp.moveaxis(tiles, 0, dim)
    dims = tiles.shape
    return tiles.reshape(*dims[:dim], dims[dim] * dims[dim + 1], *dims[dim + 2 :])


def sent_to_all(value, axis):
    devices = lax.axis_size(axis)
    return lax.all_to_all(
        jnp.broadcast_to(value[None], (devices, *value.shape)), axis, 0, 0, tiled=True
    )


def gather_directly(value, axis, dim):
    return laid_out(sent_to_all(value, axis), dim)


def gather_in_order(value, axes, turns):
    tiles = value
    for k in turns:
        tiles = lax.all_gather(tiles, axes[k])
    done = turns[::-1]
    back = [done.index(k) for k in range(len(axes))]
    tiles = tiles.transpose(*back, *range(len(axes), tiles.ndim))
    return tiles.reshape(-1, *value.shape)


def gather_axes(value, axes, turns, dim):
    return laid_out(gather_in_order(value, axes, turns), dim)


def retrace(qvals, rewards, actions, done_flags, behaviour):
    seqs = rewards.shape[0]
    length = rewards.shape[1]
    actcount = qvals.shape[1]
    qvals = qvals.reshape(seqs, length, actcount)
    probs = jax.nn.softmax(4.0 * qvals, axis=-1)
    value = jnp.sum(probs * qvals, axis=-1)
    onehot = (actions[:, :, None] == jnp.arange(actcount, dtype=jnp.int32)[None, None, :]).astype(
        jnp.float32
    )
    taken = jnp.sum(onehot * qvals, axis=-1)
    chosen = jnp.sum(onehot * probs, axis=-1)
    trace = 0.95 * jnp.minimum(1.0, chosen / behaviour)
    keep = 0.99 * (1.0 - done_flags.astype(jnp.float32))

    def stepper(later, inputs):
        reward_t, keep_t, value_n, trace_n, taken_n = inputs
        now = reward_t + keep_t * (value_n + trace_n * (later - taken_n))
        return (now, now)

    inputs = (rewards[:, :-1].T, keep[:, :-1].T, value[:, 1:].T, trace[:, 1:].T, taken[:, 1:].T)
    last = taken[:, length - 1]
    final, earlier = lax.scan(stepper, last, inputs, reverse=True)
    return jnp.concatenate([earlier.T, last[:, None]], axis=1)


def per_device(observations, layer_weights, head_weights, rewards, actions, done_flags, behaviour):
    layers = layer_weights.shape[0]
    hidden = lax.all_to_all(observations, "mp", split_axis=0, concat_axis=1, tiled=True)
    for layer in range(layers):
        widened = gather_directly(layer_weights[layer], "mp", 1)
        complete = gather_axes(widened, DP, (0, 1, 2), 0)
        summed = jnp.dot(hidden, complete, preferred_element_type=jnp.float32)
        hidden = jax.nn.relu(summed).astype(jnp.bfloat16)
    whole_head = gather_directly(head_weights, "mp", 0)
    qvals = jnp.dot(hidden, whole_head, preferred_element_type=jnp.float32)
    share = rewards.shape[0] // lax.axis_size("mp")
    offset = lax.axis_index("mp") * share
    local = retrace(
        qvals,
        lax.dynamic_slice_in_dim(rewards, offset, share, 0),
        lax.dynamic_slice_in_dim(actions, offset, share, 0),
        lax.dynamic_slice_in_dim(done_flags, offset, share, 0),
        lax.dynamic_slice_in_dim(behaviour, offset, share, 0),
    )
    return gather_directly(local, "mp", 0)


def solution(mesh):
    split = Mesh(mesh.devices.reshape(2, 8, 4, mesh.shape["mp"]), ("dp_0", "dp_1", "dp_2", "mp"))
    placed = (
        P(DP, "mp"),
        P(None, DP, "mp"),
        P("mp", None),
        P(DP, None),
        P(DP, None),
        P(DP, None),
        P(DP, None),
    )
    return jax.shard_map(
        per_device, mesh=split, in_specs=placed, out_specs=P(DP, None), check_vma=False
    )
```

profile of v0, /device:TPU:1, one launch (start us, length us, event | category | flops | bytes accessed | tf_op | source)
XLA Modules:
  0.0 375.6 jit_solution(12270167339554008198)
XLA Ops:
  6.5 0.8 slice_bitcast_fusion
  7.3 9.1 %all_to_all.39 = bf16[4,32,512]{2,1,0:T(8,128)(2,1)S(1)} all-to-all(bf16[4,32,512]{2,1,0:T(8,128)(2,1)S(1)} %broadcast_in_dim.44), channel_id=1, replica_groups=mesh['dp_0'=2,'dp_1'=8,'dp_2'=4,'mp'=4] {'mp'}, dimensions={0} | all-to-all | bytes 262144 | tf_op jit(solution)/shard_map/all_to_all | solution.py:18
  16.7 6.1 %all_gather.30 = bf16[2,32,2048]{2,1,0:T(8,128)(2,1)} all-gather(bf16[1,32,2048]{2,1,0:T(8,128)(2,1)S(1)} %all_gather_reshape.6), channel_id=1, replica_groups=mesh['dp_0'=2,'dp_1'=8,'dp_2'=4,'mp'=4] {'dp_0'}, dimensions={0}, use_global_device_ids=true | all-gather | bytes 393216 | tf_op jit(solution)/shard_map/all_gather | solution.py:30
  22.9 8.1 %all_to_all.40 = bf16[4,32,512]{2,1,0:T(8,128)(2,1)S(1)} all-to-all(bf16[4,32,512]{2,1,0:T(8,128)(2,1)S(1)} %broadcast_in_dim.46), channel_id=1, replica_groups=mesh['dp_0'=2,'dp_1'=8,'dp_2'=4,'mp'=4] {'mp'}, dimensions={0} | all-to-all | bytes 262144 | tf_op jit(solution)/shard_map/all_to_all | solution.py:18
  31.2 6.1 %all_gather.35 = bf16[2,32,2048]{2,1,0:T(8,128)(2,1)} all-gather(bf16[1,32,2048]{2,1,0:T(8,128)(2,1)S(1)} %all_gather_reshape.7), channel_id=1, replica_groups=mesh['dp_0'=2,'dp_1'=8,'dp_2'=4,'mp'=4] {'dp_0'}, dimensions={0}, use_global_device_ids=true | all-gather | bytes 393216 | tf_op jit(solution)/shard_map/all_gather | solution.py:30
  37.4 25.0 %all-gather.9.cloned.1.call-done = bf16[16,32,2048]{2,1,0:T(8,128)(2,1)} async-done(((bf16[2,32,2048]{2,1,0:T(8,128)(2,1)}), bf16[16,32,2048]{2,1,0:T(8,128)(2,1)}) %all-gather.9.cloned.1.call-update) | async-done | bytes 2097168 | tf_op jit(solution)/shard_map/all_gather | solution.py:30
  62.5 41.2 %all-gather.13.cloned.1.call-done = bf16[16,32,2048]{2,1,0:T(8,128)(2,1)} async-done(((bf16[2,32,2048]{2,1,0:T(8,128)(2,1)}), bf16[16,32,2048]{2,1,0:T(8,128)(2,1)}) %all-gather.13.cloned.1.call-update) | async-done | bytes 2097168 | tf_op jit(solution)/shard_map/all_gather | solution.py:30
  103.7 10.8 %all_to_all.41 = bf16[4,512,18]{1,2,0:T(8,128)(2,1)S(1)} all-to-all(bf16[4,512,18]{1,2,0:T(8,128)(2,1)S(1)} %broadcast_in_dim.47), channel_id=1, replica_groups=mesh['dp_0'=2,'dp_1'=8,'dp_2'=4,'mp'=4] {'mp'}, dimensions={0} | all-to-all | bytes 147456 | tf_op jit(solution)/shard_map/all_to_all | solution.py:18
  114.5 4.6 %all-to-all-start = ((bf16[4,832,512]{2,1,0:T(8,128)(2,1)}), bf16[4,832,512]{2,1,0:T(8,128)(2,1)S(1)}, u32[]{:S(2)}, u32[]{:S(2)}) async-start(bf16[4,832,512]{2,1,0:T(8,128)(2,1)} %bitcast.88), calls=%async_computation | async-start | bytes 6815744 | tf_op jit(solution)/shard_map/all_to_all | solution.py:69
  119.1 0.7 constant_dynamic-slice_fusion.5
  121.2 0.9 reshape.22
  122.1 35.8 %all-to-all-done = bf16[4,832,512]{2,1,0:T(8,128)(2,1)S(1)} async-done(((bf16[4,832,512]{2,1,0:T(8,128)(2,1)}), bf16[4,832,512]{2,1,0:T(8,128)(2,1)S(1)}, u32[]{:S(2)}, u32[]{:S(2)}) %all-to-all-start) | async-done | bytes 3407904 | tf_op jit(solution)/shard_map/all_to_all | solution.py:69
  158.0 2.3 copy.50
  160.3 33.4 %all-gather.11.cloned.1.call-done = bf16[32,2,32,2048]{3,2,1,0:T(8,128)(2,1)} async-done(((bf16[8,2,32,2048]{3,2,1,0:T(8,128)(2,1)}), bf16[32,2,32,2048]{3,2,1,0:T(8,128)(2,1)}) %all-gather.11.cloned.1.call-update) | async-done | bytes 8388624 | tf_op jit(solution)/shard_map/all_gather | solution.py:30
  193.7 8.3 %copy.38 = bf16[2,8,4,32,2048]{4,3,2,1,0:T(8,128)(2,1)} copy(bf16[2,8,4,32,2048]{4,3,0,1,2:T(8,128)(2,1)} %bitcast.84) | data formatting | bytes 16777216 | tf_op jit(solution)/shard_map/transpose | solution.py:33
  201.9 80.0 %all-gather.15.cloned.1.call-done = bf16[32,2,32,2048]{3,2,1,0:T(8,128)(2,1)} async-done(((bf16[8,2,32,2048]{3,2,1,0:T(8,128)(2,1)}), bf16[32,2,32,2048]{3,2,1,0:T(8,128)(2,1)}) %all-gather.15.cloned.1.call-update) | async-done | bytes 8388624 | tf_op jit(solution)/shard_map/all_gather | solution.py:30
  282.0 8.4 %copy.40 = bf16[2,8,4,32,2048]{4,3,2,1,0:T(8,128)(2,1)} copy(bf16[2,8,4,32,2048]{4,3,0,1,2:T(8,128)(2,1)} %bitcast.85) | data formatting | bytes 16777216 | tf_op jit(solution)/shard_map/transpose | solution.py:33
  290.4 9.8 %maximum_convert_fusion.1 = bf16[832,2048]{1,0:T(8,128)(2,1)S(1)} fusion(bf16[832,2048]{1,0:T(8,128)(2,1)S(1)} %bitcast.89, bf16[2048,2048]{1,0:T(8,128)(2,1)} %bitcast.86), kind=kOutput, calls=%fused_computation.18 | convolution fusion | flops 6982729728 | bytes 15204352 | tf_op jit(solution)/shard_map/dot_general | solution.py:73
  300.2 7.4 %maximum_convert_fusion = bf16[832,2048]{1,0:T(8,128)(2,1)S(1)} fusion(bf16[832,2048]{1,0:T(8,128)(2,1)S(1)} %maximum_convert_fusion.1, bf16[2048,2048]{1,0:T(8,128)(2,1)S(1)} %bitcast.87), kind=kOutput, calls=%fused_computation.17 | convolution fusion | flops 6982729728 | bytes 15204352 | tf_op jit(solution)/shard_map/dot_general | solution.py:73
  307.6 3.3 select_reduce_fusion
  311.1 0.8 slice_bitcast_fusion.2
  312.1 0.8 fusion.21
  313.1 47.2 %while.16 = (s32[]{:T(128)}, f32[13]{0:T(128)S(1)}, f32[63,13]{1,0:T(8,128)S(1)}, f32[63,13]{1,0:T(8,128)}, f32[63,13]{1,0:T(8,128)S(1)}, /*index=5*/f32[63,13]{...) while((s32[]{:T(128)}, f32[13]{0:T(128)S(1)}, ...), condition=%wide.region_6.7_spmd, body=%wide.region_5.6_spmd.sunk | while | flops 68 | bytes 597 | solution.py:63
  330.3 0.7 fusion.42
  331.1 0.7 fusion.42
  331.9 0.7 fusion.42
  332.6 0.7 fusion.42
  333.4 0.7 fusion.42
  334.1 0.7 fusion.42
  334.9 0.7 fusion.42
  335.6 0.7 fusion.42
  360.6 6.5 %all_to_all.42 = f32[4,1,832]{2,1,0:T(1,128)S(1)} all-to-all(f32[4,1,832]{2,1,0:T(1,128)S(1)} %reshape.25), channel_id=1, replica_groups=mesh['dp_0'=2,'dp_1'=8,'dp_2'=4,'mp'=4] {'mp'}, dimensions={0} | all-to-all | bytes 26624 | tf_op jit(solution)/shard_map/all_to_all | solution.py:18
  (158 shorter events, 45.4 us)
Async XLA Ops:
  6.5 114.0 %copy-start = (s32[52,64]{1,0:T(8,128)S(1)}, s32[52,64]{1,0:T(8,128)}, u32[]{:S(2)}) copy-start(s32[52,64]{1,0:T(8,128)} %param.13) | copy-start | bytes 39940
  6.5 55.9 %all-gather.9.cloned.1.call-start = ((), (), s32[]{:S(2)}) async-start(), calls=%async_computation.5 | async-start | bytes 2359296 | tf_op jit(solution)/shard_map/all_gather | solution.py:30
  16.6 87.1 %copy-start.3 = (bf16[512,18]{0,1:T(8,128)(2,1)S(1)}, bf16[512,18]{0,1:T(8,128)(2,1)}, u32[]{:S(2)}) copy-start(bf16[512,18]{0,1:T(8,128)(2,1)} %param.11) | copy-start | bytes 55300
  22.8 80.8 %all-gather.13.cloned.1.call-start = ((), (), s32[]{:S(2)}) async-start(), calls=%async_computation.7 | async-start | bytes 2359296 | tf_op jit(solution)/shard_map/all_gather | solution.py:30
  37.3 156.3 %all-gather.11.cloned.1.call-start = ((), (), s32[]{:S(2)}) async-start(), calls=%async_computation.6 | async-start | bytes 10485760 | tf_op jit(solution)/shard_map/all_gather | solution.py:30
  62.4 219.5 %all-gather.15.cloned.1.call-start = ((), (), s32[]{:S(2)}) async-start(), calls=%async_computation.8 | async-start | bytes 10485760 | tf_op jit(solution)/shard_map/all_gather | solution.py:30
  114.5 43.5 %all-to-all-start = ((bf16[4,832,512]{2,1,0:T(8,128)(2,1)}), bf16[4,832,512]{2,1,0:T(8,128)(2,1)S(1)}, u32[]{:S(2)}, u32[]{:S(2)}) async-start(bf16[4,832,512]{2,1,0:T(8,128)(2,1)} %bitcast.88), calls=%async_computation | async-start | bytes 6815744 | tf_op jit(solution)/shard_map/all_to_all | solution.py:69
  282.0 8.4 %copy-start.2 = (bf16[4,104,8,512]{3,2,0,1:T(8,128)(2,1)S(1)}, bf16[4,104,8,512]{3,2,0,1:T(8,128)(2,1)}, u32[]{:S(2)}) copy-start(bf16[4,104,8,512]{3,2,0,1:T(8,128)(2,1)} %copy.50) | copy-start | bytes 10223620
  290.4 9.8 %copy-start.1 = (bf16[2,8,4,32,2048]{4,3,2,1,0:T(8,128)(2,1)S(1)}, bf16[2,8,4,32,2048]{4,3,2,1,0:T(8,128)(2,1)}, u32[]{:S(2)}) copy-start(bf16[2,8,4,32,2048]{4,3,2,1,0:T(8,128)(2,1)} %copy.40) | copy-start | bytes 25165828
Sparse Core Ops, SparseCore 0:
  22.9 39.4 all-gather.8
  64.2 39.4 all-gather.12
  105.5 88.1 all-gather.10
  195.3 86.5 all-gather.14
where the time goes:
time: 378 us; the launch traced here: 376 us
  waiting for transfers between devices  216 us (57%)
  blocking collectives  46.8 us (12%)
  other arithmetic  45.8 us (12%)
  local copies, waits for them, and re-layouts  28.1 us (7%)
  matrix products  20.5 us (5%)
  between operations  13.2 us (3%)
  starting transfers between devices  4.77 us (1%)
    all_gather x4, waiting for transfers between devices, gather_in_order(): tiles = lax.all_gather(tiles, axes[k])  180 us
    add x63, other arithmetic, stepper(): now = reward_t + keep_t * (value_n + trace_n * (later - taken_n))  44.2 us
    all_to_all x1, waiting for transfers between devices, per_device(): lax.all_to_all(observations, 'mp', split_axis=0, concat_axis=1, tiled=True)  35.8 us
    all_to_all x4, blocking collectives, sent_to_all(): lax.all_to_all(jnp.broadcast_to(value[None], (devices, *value.shape)), ax...  34.6 us
    dot_general x2, matrix products, per_device(): summed = jnp.dot(hidden, complete, preferred_element_type=jnp.float32)  17.2 us
    transpose x2, local copies, waits for them, and re-layouts, gather_in_order(): tiles = tiles.transpose(*back, *range(len(axes), tiles.ndim))  16.7 us
    all_gather x2, blocking collectives, gather_in_order(): tiles = lax.all_gather(tiles, axes[k])  12.2 us
  transfers between devices with their start and end apart: 5, of which 5 were waited for; matrix products, arithmetic and copies ran while one was open for 4% of the time, Pallas kernels for 0%

commit v1 on v0

v1 whole, which is shorter than its diff:
```python
import jax
import jax.numpy as jnp
from jax import lax
from jax.experimental import pallas as pl
from jax.experimental.pallas import tpu as pltpu
from jax.sharding import Mesh
from jax.sharding import PartitionSpec as P

MESH = pl.DeviceIdType.MESH
AXES = ("yh", "z", "x", "yl", "core")
DP = ("yh", "z", "x")
MP = ("yl", "core")
NX, NZ = 4, 8
CHUNKS = 4
GAP = 2

SLOTS = (
    ((0, 0, 0), (1, 0, 0), (2, 0, 0), (3, 0, 0), (4, 0, 0)),
    ((0, 1, 0), (1, 1, 0), (2, 1, 0), (3, 1, 0), (4, 1, 0)),
    ((0, 0, 24), (1, 0, 7), (2, 0, 7), (3, 0, 32), (4, 0, 7)),
    ((0, 0, 8), (1, 0, 8), (2, 0, 1), (3, 0, 8), (4, 0, 32)),
    ((0, 0, 6), (1, 0, 15), (2, 0, 33), (3, 0, 1), (4, 0, 56)),
    ((0, 0, 15), (1, 0, 6), (2, 0, 25), (3, 0, 33), (4, 0, 6)),
    ((0, 0, 23), (1, 0, 38), (2, 0, 57), (3, 0, 57), (4, 0, 23)),
    ((0, 0, 5), (1, 0, 33), (2, 0, 38), (3, 0, 34), (4, 0, 5)),
    ((0, 0, 16), (1, 0, 34), (2, 0, 58), (3, 0, 58), (4, 0, 55)),
    ((0, 0, 62), (1, 0, 37), (2, 0, 4), (3, 0, 35), (4, 0, 62)),
    ((0, 0, 42), (1, 0, 5), (2, 0, 59), (3, 0, 59), (4, 0, 22)),
    ((0, 0, 61), (1, 0, 4), (2, 0, 61), (3, 0, 42), (4, 0, 45)),
    ((0, 0, 51), (1, 0, 10), (2, 0, 2), (3, 0, 51), (4, 0, 21)),
    ((0, 0, 35), (1, 1, 32), (2, 1, 1), (3, 0, 10), (4, 0, 28)),
    ((0, 1, 1), (1, 1, 7), (2, 1, 24), (3, 1, 1), (4, 1, 7)),
    ((0, 1, 25), (1, 1, 40), (2, 1, 25), (3, 1, 25), (4, 1, 40)),
    ((0, 1, 2), (1, 1, 2), (2, 1, 6), (3, 1, 40), (4, 1, 6)),
    ((0, 1, 26), (1, 1, 47), (2, 1, 26), (3, 1, 48), (4, 1, 47)),
    ((0, 1, 30), (1, 1, 34), (2, 1, 30), (3, 1, 26), (4, 1, 30)),
    ((0, 1, 5), (1, 1, 5), (2, 1, 58), (3, 1, 58), (4, 1, 55)),
    ((0, 1, 29), (1, 1, 15), (2, 1, 27), (3, 1, 42), (4, 1, 22)),
    ((0, 1, 13), (1, 1, 6), (2, 1, 59), (3, 1, 59), (4, 1, 54)),
    ((0, 1, 6), (1, 1, 1), (2, 1, 7), (3, 1, 43), (4, 1, 13)),
    ((0, 1, 7), (1, 1, 60), (2, 1, 32), (3, 1, 51), (4, 1, 21)),
    ((0, 1, 31), (1, 1, 59), (2, 1, 12), (3, 1, 10), (4, 1, 29)),
    ((3, 1, 2),),
)
STEPS = ((1, 0, 0), (0, 1, 0), (0, 3, 0), (0, 0, 1), (0, 0, 7))


def split(code):
    return code // 32, code // 8 % 4, code % 8


def moved(code, link):
    pair, dx, dz = split(code)
    a, b, c = STEPS[link]
    return ((pair + a) % 2 * 4 + (dx + b) % 4) * 8 + (dz + c) % 8


def kernel(
    obs, own_w, own_head, rewards, actions, done, behaviour, out,
    wg, xb, h1, heads, lanes, cols, tsend, trecv,
    w_recv, i_recv, d_recv, i_send, r_send, d_send,
    o_recv, o_send, o_local, h_recv, h_send, t_recv, t_send,
):
    yh, z, x = lax.axis_index("yh"), lax.axis_index("z"), lax.axis_index("x")
    yl, core = lax.axis_index("yl"), lax.axis_index("core")
    rows_all, width = xb.shape
    depth, part = own_w.shape[1], own_w.shape[2]
    seqs, length = rows_all // rewards.shape[1], rewards.shape[1]
    step_rows = rows_all // CHUNKS
    acts = own_head.shape[0]
    packets = 2 * NX * NZ

    xp, xm = lax.rem(x + 1, NX), lax.rem(x + NX - 1, NX)
    zp, zm = lax.rem(z + 1, NZ), lax.rem(z + NZ - 1, NZ)
    links = (
        {"yh": 1 - yh, "yl": 1 - yl},
        {"x": xp},
        {"x": xm},
        {"z": zp},
        {"z": zm},
    )
    peers = (None, {"core": 1 - core}, {"yl": 1 - yl}, {"yl": 1 - yl, "core": 1 - core})
    mine = yl * 2 + core
    peer_mp = (
        mine,
        yl * 2 + (1 - core),
        (1 - yl) * 2 + core,
        (1 - yl) * 2 + (1 - core),
    )

    y_from = (yh, 1 - yh)
    x_from = tuple(lax.rem(x + NX - k, NX) for k in range(NX))
    z_from = tuple(lax.rem(z + NZ - k, NZ) for k in range(NZ))

    def rows_of(code):
        a, b, c = split(code)
        start = ((y_from[a] * NZ + z_from[c]) * NX + x_from[b]) * depth
        return pl.ds(pl.multiple_of(start, depth), depth)

    own_rows = rows_of(0)

    def whole(layer, code, side):
        return wg.at[layer, side, :, rows_of(code), :]

    def half(layer, which):
        return wg.at[layer, core, which, own_rows, :]

    barrier = pltpu.get_barrier_semaphore()
    for target in links + peers[1:]:
        pl.semaphore_signal(barrier, inc=1, device_id=target, device_id_type=MESH)
    pl.semaphore_wait(barrier, len(links) + 3)

    def remote(src, dst, send, recv, target):
        return pltpu.make_async_remote_copy(
            src_ref=src, dst_ref=dst, send_sem=send, recv_sem=recv,
            device_id=target, device_id_type=MESH,
        )

    def forward(layer, ref):
        remote(ref, ref, d_send.at[layer], d_recv.at[layer], peers[1]).start()

    for layer in range(2):
        remote(own_w.at[layer], half(layer, yl), i_send.at[layer], i_recv.at[layer], peers[2]).start()
    for slot in SLOTS[:2]:
        for link, layer, code in slot:
            assert code == 0
            remote(
                own_w.at[layer], half(layer, yl), r_send.at[layer],
                w_recv.at[layer, moved(0, link)], links[link],
            ).start()
    for m in range(1, 4):
        remote(own_head, heads.at[mine], h_send.at[m], h_recv.at[m], peers[m]).start()
    for layer in range(2):
        remote(
            own_w.at[layer], half(layer, yl), d_send.at[layer], d_recv.at[layer], peers[1]
        ).start()

    my_cols = pl.ds(pl.multiple_of(mine * part, part), part)

    def chunk_of(m, k):
        start = peer_mp[m] * rows_all + k * step_rows
        return obs.at[pl.ds(pl.multiple_of(start, step_rows), step_rows), :]

    for k in range(CHUNKS):
        here = pl.ds(k * step_rows, step_rows)
        pltpu.make_async_copy(chunk_of(0, k), xb.at[here, my_cols], o_local.at[k]).start()
        for m in (2, 3, 1):
            remote(
                chunk_of(m, k), xb.at[here, my_cols], o_send.at[m], o_recv.at[m, k], peers[m]
            ).start()

    for layer in range(2):
        wg[layer, core, yl, own_rows, :] = own_w[layer]
    heads[mine] = own_head[...]

    first = mine * seqs
    for s in range(seqs):
        lanes[0:1, s * length : (s + 1) * length] = actions[pl.ds(first + s, 1), :]
        cols[3, s : s + 1, :length] = behaviour[pl.ds(first + s, 1), :]
        cols[4, s : s + 1, :length] = rewards[pl.ds(first + s, 1), :]
        cols[5, s : s + 1, :length] = 0.99 * (
            1.0 - done[pl.ds(first + s, 1), :].astype(jnp.float32)
        )

    for layer in range(2):
        ref = half(layer, 1 - yl)
        remote(ref, ref, i_send.at[layer], i_recv.at[layer], peers[2]).wait_recv()
        for link, at, code in SLOTS[layer]:
            assert at == layer
            remote(
                ref, ref, r_send.at[layer], w_recv.at[layer, moved(0, link)], links[link]
            ).start()
        forward(layer, ref)

    def arrive(slot):
        for link, layer, code in slot:
            got = moved(code, link)
            ref = whole(layer, got, core)
            remote(ref, ref, r_send.at[layer], w_recv.at[layer, got], links[link]).wait_recv()
            forward(layer, ref)

    def send(slot):
        for link, layer, code in slot:
            ref = whole(layer, code, core)
            remote(
                ref, ref, r_send.at[layer], w_recv.at[layer, moved(code, link)], links[link]
            ).start()

    def partner_done(layer):
        ref = wg.at[layer, 1 - core]
        remote(ref, ref, d_send.at[layer], d_recv.at[layer], peers[1]).wait_recv()

    def chunk_done(k):
        here = pl.ds(k * step_rows, step_rows)
        dst = xb.at[here, my_cols]
        pltpu.make_async_copy(chunk_of(0, k), dst, o_local.at[k]).wait()
        for m in (1, 2, 3):
            dst = xb.at[here, pl.ds(pl.multiple_of(peer_mp[m] * part, part), part)]
            remote(dst, dst, o_send.at[m], o_recv.at[m, k], peers[m]).wait_recv()

    def first_layer(k):
        here = pl.ds(k * step_rows, step_rows)

        def column(j, carry):
            c, y = j // 2, j % 2
            total = jnp.dot(xb[here, :], wg[0, c, y], preferred_element_type=jnp.float32)
            place = pl.ds(pl.multiple_of((y * 2 + c) * part, part), part)
            h1[here, place] = jnp.maximum(total, 0.0).astype(jnp.bfloat16)
            return carry

        lax.fori_loop(0, 4, column, 0)

    last0 = max(t for t, slot in enumerate(SLOTS) if any(at == 0 for _, at, _ in slot))
    end = len(SLOTS)
    compute_at = {last0 + GAP + 1 + n * 3: n for n in range(CHUNKS)}
    todo = 0
    for t in range(2, end + GAP):
        if t >= GAP:
            arrive(SLOTS[t - GAP])
        if t < end:
            send(SLOTS[t])
        if t in compute_at:
            k = compute_at[t]
            if k == 0:
                partner_done(0)
            chunk_done(k)
            first_layer(k)
            todo = k + 1
    for k in range(todo, CHUNKS):
        chunk_done(k)
        first_layer(k)
    partner_done(1)

    def second_layer(i, carry):
        here = pl.ds(pl.multiple_of(i * step_rows, step_rows), step_rows)
        for c in range(2):
            for y in range(2):
                total = jnp.dot(h1[here, :], wg[1, c, y], preferred_element_type=jnp.float32)
                place = pl.ds((y * 2 + c) * part, part)
                xb[here, place] = jnp.maximum(total, 0.0).astype(jnp.bfloat16)
        return carry

    lax.fori_loop(0, CHUNKS, second_layer, 0)

    for m in range(1, 4):
        dst = heads.at[peer_mp[m]]
        remote(dst, dst, h_send.at[m], h_recv.at[m], peers[m]).wait_recv()
    q = jnp.zeros((acts, rows_all), jnp.float32)
    for m in range(4):
        q += lax.dot_general(
            heads[m], xb[:, m * part : (m + 1) * part], (((1,), (1,)), ((), ())),
            preferred_element_type=jnp.float32,
        )

    peak = jnp.max(q, axis=0, keepdims=True)
    powers = jnp.exp(4.0 * (q - peak))
    probs = powers / jnp.sum(powers, axis=0, keepdims=True)
    value = jnp.sum(probs * q, axis=0, keepdims=True)
    picked = lax.broadcasted_iota(jnp.int32, (acts, rows_all), 0) == lanes[0:1, :rows_all]
    taken = jnp.sum(jnp.where(picked, q, 0.0), axis=0, keepdims=True)
    chosen = jnp.sum(jnp.where(picked, probs, 0.0), axis=0, keepdims=True)
    for s in range(seqs):
        at = slice(s * length, (s + 1) * length)
        cols[0, s : s + 1, :length] = value[:, at]
        cols[1, s : s + 1, :length] = taken[:, at]
        cols[2, s : s + 1, :length] = chosen[:, at]

    taken = cols[1]
    trace = 0.95 * jnp.minimum(1.0, cols[2] / cols[3])
    step = lax.broadcasted_iota(jnp.int32, taken.shape, 1)

    def later(a, k):
        return pltpu.roll(a, taken.shape[1] - k, 1)

    keep = cols[5]
    inner = step < length - 1
    slope = jnp.where(inner, keep * later(trace, 1), 0.0)
    base = jnp.where(
        inner,
        cols[4] + keep * (later(cols[0], 1) - later(trace * taken, 1)),
        taken,
    )
    base = jnp.where(step < length, base, 0.0)
    k = 1
    while k < length:
        base = base + slope * later(base, k)
        slope = slope * later(slope, k)
        k *= 2

    tsend[...] = base
    trecv[mine] = base
    for m in (2, 3, 1):
        remote(tsend, trecv.at[mine], t_send.at[m], t_recv.at[m], peers[m]).start()

    for layer in range(2):
        remote(own_w.at[layer], half(layer, yl), i_send.at[layer], i_recv.at[layer], peers[2]).wait_send()
        ref = wg.at[layer, 0, :, pl.ds(0, (packets - 1) * depth), :]
        remote(ref, ref, r_send.at[layer], d_recv.at[layer], peers[1]).wait_send()
        ref = wg.at[layer, 0]
        remote(ref, ref, d_send.at[layer], d_recv.at[layer], peers[1]).wait_send()
    for m in range(1, 4):
        dst = xb.at[:, my_cols]
        src = obs.at[pl.ds(0, rows_all), :]
        remote(src, dst, o_send.at[m], o_recv.at[m, 0], peers[m]).wait_send()
        remote(own_head, heads.at[mine], h_send.at[m], h_recv.at[m], peers[m]).wait_send()
    for m in (1, 2, 3):
        dst = trecv.at[peer_mp[m]]
        remote(tsend, dst, t_send.at[m], t_recv.at[m], peers[m]).wait()
    for m in range(4):
        out[m * seqs : (m + 1) * seqs, :] = trecv[m, :seqs, :length]


def per_device(obs, layers, head, rewards, actions, done, behaviour):
    depth, part = layers.shape[1], layers.shape[2]
    rows_all, width = obs.shape[0] // 4, part * 4
    acts = head.shape[1]
    dma = pltpu.SemaphoreType.DMA
    vmem = pl.BlockSpec(memory_space=pltpu.VMEM)
    lanes = -(-rows_all // 128) * 128
    return pl.pallas_call(
        kernel,
        out_shape=jax.ShapeDtypeStruct(rewards.shape, jnp.float32),
        in_specs=[pl.BlockSpec(memory_space=pl.ANY)] + [vmem] * 6,
        out_specs=vmem,
        scratch_shapes=[
            pltpu.VMEM((2, 2, 2, width, part), jnp.bfloat16),
            pltpu.VMEM((rows_all, width), jnp.bfloat16),
            pltpu.VMEM((rows_all, width), jnp.bfloat16),
            pltpu.VMEM((4, acts, part), jnp.bfloat16),
            pltpu.VMEM((8, lanes), jnp.int32),
            pltpu.VMEM((6, 16, 128), jnp.float32),
            pltpu.VMEM((16, 128), jnp.float32),
            pltpu.VMEM((4, 16, 128), jnp.float32),
            dma((2, 2 * NX * NZ)),
            dma((2,)), dma((2,)), dma((2,)), dma((2,)), dma((2,)),
            dma((4, CHUNKS)), dma((4,)), dma((CHUNKS,)),
            dma((4,)), dma((4,)), dma((4,)), dma((4,)),
        ],
        compiler_params=pltpu.CompilerParams(
            collective_id=0, has_side_effects=True, vmem_limit_bytes=60 * 2**20
        ),
    )(obs, layers, head.T, rewards, actions, done, behaviour)


def solution(mesh):
    devices = mesh.devices.reshape(2, NZ, NX, 2, 2)
    laid = Mesh(devices, AXES)
    placed = (
        P(DP, MP),
        P(None, DP, MP),
        P(MP, None),
        P(DP, None),
        P(DP, None),
        P(DP, None),
        P(DP, None),
    )
    return jax.shard_map(
        per_device, mesh=laid, in_specs=placed, out_specs=P(DP, None), check_vma=False
    )
```

time: 378 us -> 85.9 us (0.23)
  waiting for transfers between devices: 216 us -> 0 us
  Pallas kernels: 0 us -> 84.3 us
  blocking collectives: 46.8 us -> 0 us
  other arithmetic: 45.8 us -> 0 us
  local copies, waits for them, and re-layouts: 28.1 us -> 1.36 us
  matrix products: 20.5 us -> 0 us
  between operations: 13.2 us -> 0.01 us
  starting transfers between devices: 4.77 us -> 0 us
    all_gather x4 -> x0, waiting for transfers between devices: 180 us -> none  [gather_in_order(): tiles = lax.all_gather(tiles, axes[k])]
    pallas_call x0 -> x1, Pallas kernels: none -> 84.3 us  [per_device(): pl.pallas_call(kernel, out_shape=jax.ShapeDtypeStruct(rewards.shape, jnp....]
    add x63 -> x0, other arithmetic: 44.2 us -> none  [stepper(): now = reward_t + keep_t * (value_n + trace_n * (later - taken_n))]
    all_to_all x1 -> x0, waiting for transfers between devices: 35.8 us -> none  [per_device(): lax.all_to_all(observations, 'mp', split_axis=0, concat_axis=1, tiled=True)]
    all_to_all x4 -> x0, blocking collectives: 34.6 us -> none  [sent_to_all(): lax.all_to_all(jnp.broadcast_to(value[None], (devices, *value.shape)), ax...]
    transpose x5 -> x0, local copies, waits for them, and re-layouts: 17.7 us -> none  [the longest x2 16.7 us: gather_in_order(): tiles = tiles.transpose(*back, *range(len(axes), tiles.ndim))]
    dot_general x2 -> x0, matrix products: 17.2 us -> none  [per_device(): summed = jnp.dot(hidden, complete, preferred_element_type=jnp.float32)]
    all_gather x2 -> x0, blocking collectives: 12.2 us -> none  [gather_in_order(): tiles = lax.all_gather(tiles, axes[k])]
  transfers between devices with their start and end apart: 5 -> 0, of which waited for: 5 -> 0; matrix products, arithmetic and copies ran while one was open for 4% -> 0% of each run, Pallas kernels for 0% -> 0%
where the time goes in v1:
time: 85.9 us; the launch traced here: 85.7 us
  Pallas kernels  84.3 us (98%)
  local copies, waits for them, and re-layouts  1.36 us (2%)
    pallas_call x1, Pallas kernels, per_device(): pl.pallas_call(kernel, out_shape=jax.ShapeDtypeStruct(rewards.shape, jnp....  84.3 us

profile of v1, /device:TPU:1, one launch (start us, length us, event | category | flops | bytes accessed | tf_op | source)
XLA Modules:
  0.0 85.7 jit_solution(870259465429792471)
XLA Ops:
  0.0 84.3 %shard_map.73 = f32[52,64]{1,0:T(8,128)} custom-call(bf16[3328,512]{1,0:T(8,128)(2,1)} %obs.1, bf16[2,32,512]{2,1,0:T(8,128)(2,1)} %own_w.1, bf16[18,512]{1,0:T(8,128)(2,1)} %bitcast.1, f32[52,64]{1,0:T(8,128)} %rewards.1, s32[52,64]{1,0:T(8,128)} %actions.1, s32[52,64]{1,0:T(8,128)} %done.1, f32[52,64]{1,0:T(8,128)} %behaviour.1), custom_call_target="tpu_custom_call" | custom-call | tf_op jit(solution)/shard_map/pallas_call | solution.py:320
  84.3 1.4 %copy.9 = f32[52,64]{1,0:T(8,128)} copy(f32[52,64]{1,0:T(8,128)} %shard_map.73) | data formatting | bytes 26624
